TPU v7x, 256 devices: a 2x2x32 block of a 4x8x32 slice. The times are simulated.
256 devices in a mesh: group: 4 (over y, x), space: 64 (over z, core).
Axes of the slice: x: 2, y: 2, z: 32, core: 2. Of those that a mesh axis runs over, the one named last changes fastest.
The devices are a block of a 4x8x32 slice.
Arguments:
- field: bfloat16 [8, 512, 512, 256], P('group', 'space'), parts along dimension 0, may hold values from -6 to 6
- spectral_weight: bfloat16 [1024, 2, 256, 256], P('space'), may hold values from -5 to 5
- skip_weight: bfloat16 [256, 256], replicated, may hold values from -0.375 to 0.375
Outputs:
- layer_out: bfloat16 [8, 512, 512, 256], P('group', 'space'), parts along dimension 0
There are 4 independent parts, one for each index of `group`. A program takes and returns all parts, laid end to end along the dimension named above; an argument that names none is the same for every part. Nothing has to cross between parts.
All inputs are finite; a program needn't handle non-finite values.
Results may differ from a plain program's by a relative error of at most 0.008.
Values may be sent and summed in bfloat16 or wider, within the bound.
A program may use at most 128 MiB of HBM per device.

v0:
```python
import math

import jax
import jax.numpy as jnp
from jax import lax
from jax.sharding import Mesh
from jax.sharding import PartitionSpec as P

NX = 512
NY = 512
C = 256
KX = 32
KY = 32
SPACE = ("space_0", "space_1")


def cut_along(array, dim, length):
    before, after = (array.shape[:dim], array.shape[dim + 1 :])
    return jnp.moveaxis(array.reshape(*before, length, -1, *after), dim, 0)


def laid_out(blocks, dim):
    blocks = jnp.moveaxis(blocks, 0, dim)
    shape = blocks.shape
    return blocks.reshape(*shape[:dim], shape[dim] * shape[dim + 1], *shape[dim + 2 :])


def moved_by_axis(blocks, axes, turns):
    inside = blocks.shape[1:]
    filled = blocks.reshape(*(lax.axis_size(a) for a in axes), *inside)
    for k in turns:
        filled = lax.all_to_all(filled, axes[k], k, k, tiled=True)
    return filled.reshape(-1, *inside)


def two_step_exchange(array, groups, turns, split_dim, concat_dim):
    length = lax.axis_size(groups[0]) * lax.axis_size(groups[1])
    blocks = cut_along(array, split_dim, length)
    return laid_out(moved_by_axis(blocks, groups, turns), concat_dim)


def stacked_from(array, axes, turns):
    blocks = array
    for k in turns:
        blocks = lax.all_gather(blocks, axes[k])
    done = turns[::-1]
    back = [done.index(k) for k in range(len(axes))]
    blocks = blocks.transpose(*back, *range(len(axes), blocks.ndim))
    return blocks.reshape(-1, *array.shape)


def gather_axes(array, axes, turns, dim):
    return laid_out(stacked_from(array, axes, turns), dim)


def wave_table(kept_index, positions, length, kept, sign):
    frequency = jnp.where(kept_index < kept // 2, kept_index, length - kept + kept_index)
    phase = frequency[:, None] * positions[None, :] % length
    angle = 2.0 * math.pi / length * phase.astype(jnp.float32)
    factor = length ** (-0.5)
    return (jnp.cos(angle) * factor, sign * jnp.sin(angle) * factor)


def shards(field, spectral_weight, skip_weight):
    highest = lax.Precision.HIGHEST
    devices = lax.axis_size(SPACE)
    position = lax.axis_index(SPACE)
    local_rows = field.shape[1]
    owned_modes = spectral_weight.shape[0]
    narrow = C // devices
    first_rows = position * local_rows + jnp.arange(local_rows, dtype=jnp.int32)
    skip_part = jnp.dot(
        field.reshape(-1, C), skip_weight, preferred_element_type=jnp.float32
    ).reshape(field.shape)
    fy_re, fy_im = wave_table(
        jnp.arange(KY, dtype=jnp.int32), jnp.arange(NY, dtype=jnp.int32), NY, KY, -1.0
    )
    fy_table = jnp.concatenate([fy_re, fy_im], axis=0).astype(jnp.bfloat16)
    split_field = field.reshape(2, local_rows, NY, devices, narrow)
    ypart = jnp.einsum("ky,sxync->sxnkc", fy_table, split_field, preferred_element_type=jnp.float32)
    ysplit_re = ypart[0, :, :, :KY] - ypart[1, :, :, KY:]
    ysplit_im = ypart[1, :, :, :KY] + ypart[0, :, :, KY:]
    outgoing = jnp.stack([ysplit_re, ysplit_im]).reshape(2, local_rows, devices, KY * narrow)
    pencil = lax.all_to_all(
        outgoing.astype(jnp.bfloat16), SPACE, split_axis=2, concat_axis=1, tiled=True
    ).astype(outgoing.dtype)
    fx_re, fx_im = wave_table(
        jnp.arange(KX, dtype=jnp.int32), jnp.arange(NX, dtype=jnp.int32), NX, KX, -1.0
    )
    fx_table = jnp.concatenate([fx_re, fx_im], axis=0)
    xpart = jnp.einsum("kx,sxq->skq", fx_table, pencil[:, :, 0], precision=highest)
    spec_re = (xpart[0, :KX] - xpart[1, KX:]).reshape(KX, KY, narrow)
    spec_im = (xpart[1, :KX] + xpart[0, KX:]).reshape(KX, KY, narrow)
    spec_local = jnp.stack([spec_re, spec_im], axis=2).astype(jnp.bfloat16)
    sendable = spec_local.reshape(devices, owned_modes * 2 * narrow)
    received = two_step_exchange(sendable, ("space_0", "space_1"), (0, 1), 0, 0)
    spec = (
        received.reshape(devices, owned_modes, 2, narrow)
        .transpose(1, 2, 0, 3)
        .reshape(owned_modes, 2, C)
    )
    product = jnp.einsum(
        "mrc,mwco->mrwo", spec, spectral_weight, preferred_element_type=jnp.float32
    )
    mixed = jnp.stack(
        [product[:, 0, 0] - product[:, 1, 1], product[:, 0, 1] + product[:, 1, 0]], axis=1
    ).astype(jnp.bfloat16)
    gy_re, gy_im = wave_table(
        jnp.arange(KY, dtype=jnp.int32), jnp.arange(NY, dtype=jnp.int32), NY, KY, 1.0
    )
    gy_table = jnp.concatenate([gy_re.T, gy_im.T], axis=0)
    piece = gather_axes(mixed, SPACE, (0, 1), 0)
    count = piece.shape[0]
    mode_index = jnp.arange(count, dtype=jnp.int32)
    kx_index = mode_index // KY
    ky_index = mode_index % KY
    cos_part, sin_part = wave_table(kx_index, first_rows, NX, KX, 1.0)
    selector = (ky_index[:, None] == jnp.arange(KY, dtype=jnp.int32)[None, :]).astype(jnp.bfloat16)
    spread_re = cos_part.astype(jnp.bfloat16).T[:, :, None] * selector[None]
    spread_im = sin_part.astype(jnp.bfloat16).T[:, :, None] * selector[None]
    part_re = jnp.einsum("xmk,msc->sxkc", spread_re, piece, preferred_element_type=jnp.float32)
    part_im = jnp.einsum("xmk,msc->sxkc", spread_im, piece, preferred_element_type=jnp.float32)
    slab = jnp.stack([part_re[0] - part_im[1], part_re[1] + part_im[0]])
    yback = jnp.einsum("yk,sxkc->sxyc", gy_table, slab, precision=highest)
    out_re = yback[0, :, :NY] - yback[1, :, NY:]
    out_im = yback[1, :, :NY] + yback[0, :, NY:]
    return (jnp.stack([out_re, out_im]) + skip_part).astype(jnp.bfloat16)


def solution(mesh):
    finer = Mesh(mesh.devices.reshape(mesh.shape["group"], 32, 2), ("group", "space_0", "space_1"))
    in_specs = (P("group", SPACE, None, None), P(SPACE, None, None, None), P())
    out_specs = P("group", SPACE, None, None)
    return jax.shard_map(
        shards, mesh=finer, in_specs=in_specs, out_specs=out_specs, check_vma=False
    )
```

profile of v0, /device:TPU:37, one launch (start us, length us, event | category | flops | bytes accessed | tf_op | source)
XLA Modules:
  0.0 256.3 jit_solution(126428525572387243)
XLA Ops:
  6.6 0.3 cosine_multiply_fusion.1
  6.9 7.8 %copy.38 = bf16[2,8,512,256]{2,1,3,0:T(8,128)(2,1)} copy(bf16[2,8,512,256]{3,2,1,0:T(8,128)(2,1)} %param.3) | data formatting | bytes 8388608 | tf_op args[0]
  14.8 7.1 %fusion.3 = f32[2,8,64,64,4]{2,3,4,1,0:T(8,128)S(1)} fusion(bf16[2,8,512,64,4]{2,1,4,3,0:T(8,128)(2,1)} %bitcast.72, f32[32,512]{1,0:T(8,128)S(1)} %get-tuple-element.20, f32[32,512]{1,0:T(8,128)S(1)} %get-tuple-element.19), kind=kOutput, calls=%fused_computation.7 | convolution fusion | flops 268566528 | bytes 5373952 | tf_op jit(solution)/shard_map/ky,sxync->sxnkc/dot_general | solution.py:80
  21.8 0.2 fusion.7
  22.1 0.2 copy.40
  22.2 0.2 copy.41
  22.4 0.1 pad_maximum_fusion
  22.6 0.4 copy.42
  23.0 75.3 %all_to_all.25 = bf16[2,8,64,128]{3,1,0,2:T(8,128)(2,1)S(1)} all-to-all(bf16[2,8,64,128]{3,1,0,2:T(8,128)(2,1)S(1)} %copy.42), channel_id=1, replica_groups=mesh['group'=4,'space_0'=32,'space_1'=2] {'space_0','space_1'}, dimensions={2} | all-to-all | bytes 524288 | tf_op jit(solution)/shard_map/all_to_all | solution.py:84
  98.3 0.3 convolution_bitcast_fusion.3
  98.6 0.1 copy.44
  98.7 0.1 copy.45
  98.8 0.1 pad_maximum_fusion.3
  98.9 0.1 copy.47
  99.0 24.5 %all_to_all.26 = bf16[32,2,1,128]{3,1,2,0:T(2,128)(2,1)S(1)} all-to-all(bf16[32,2,1,128]{3,1,2,0:T(2,128)(2,1)S(1)} %copy.47), channel_id=1, replica_groups=mesh['group'=4,'space_0'=32,'space_1'=2] {'space_0'}, dimensions={0} | all-to-all | bytes 32768 | tf_op jit(solution)/shard_map/all_to_all | solution.py:32
  123.6 6.1 %all_to_all.27 = bf16[32,2,1,128]{3,0,2,1:T(8,128)(2,1)S(1)} all-to-all(bf16[32,2,1,128]{3,0,2,1:T(8,128)(2,1)S(1)} %copy.48), channel_id=1, replica_groups=mesh['group'=4,'space_0'=32,'space_1'=2] {'space_1'}, dimensions={1} | all-to-all | bytes 32768 | tf_op jit(solution)/shard_map/all_to_all | solution.py:32
  129.7 1.1 reshape_reshape_reshape.4
  130.8 1.0 copy.50
  131.8 0.1 copy.56
  131.9 2.8 %fusion.58 = f32[16,2,2,256]{3,1,2,0:T(2,128)S(1)} fusion(bf16[16,2,256,1]{2,1,3,0:T(2,128)(2,1)S(1)} %copy.56, bf16[16,2,256,256]{3,2,1,0:T(8,128)(2,1)} %param.4), kind=kOutput, calls=%fused_computation.102 | convolution fusion | flops 8388608 | bytes 4276224 | tf_op jit(solution)/shard_map/mrc,mwco->mrwo/dot_general | solution.py:102
  134.8 45.7 %all_gather.10 = bf16[32,16,2,256]{3,1,2,0:T(8,128)(2,1)} all-gather(bf16[1,16,2,256]{3,1,2,0:T(8,128)(2,1)S(1)} %pad_maximum_fusion.4), channel_id=1, replica_groups=mesh['group'=4,'space_0'=32,'space_1'=2] {'space_0'}, dimensions={0}, use_global_device_ids=true | all-gather | bytes 540672 | tf_op jit(solution)/shard_map/all_gather | solution.py:45
  180.6 0.2 multiply_convert_fusion.1
  180.8 0.3 cosine_multiply_fusion
  181.2 26.4 %all-gather.3.cloned.1.call-done = bf16[64,16,2,256]{3,1,2,0:T(8,128)(2,1)} async-done(((bf16[32,16,2,256]{3,1,2,0:T(8,128)(2,1)}), bf16[64,16,2,256]{3,1,2,0:T(8,128)(2,1)}) %all-gather.3.cloned.1.call-update) | async-done | bytes 1048592 | tf_op jit(solution)/shard_map/all_gather | solution.py:45
  207.6 1.3 copy.52
  209.0 0.4 convolution_bitcast_fusion.1
  209.4 0.4 convolution_bitcast_fusion.2
  209.8 0.1 slice_subtract_fusion.2
  209.9 16.0 %convolution_bitcast_fusion = f32[2,8,1024,256]{2,3,1,0:T(8,128)} fusion(f32[1,8,32,256]{3,2,1,0:T(8,128)S(1)} %get-tuple-element.10, f32[1,8,32,256]{3,2,1,0:T(8,128)S(1)} %get-tuple-element.9, f32[512,32]{0,1:T(8,128)S(1)} %get-tuple-element.18, f32[512,32]{0,1:T(8,128)S(1)} %get-tuple-element.17), kind=kOutput, calls=%fused_computation.2 | convolution fusion | flops 1610776576 | bytes 17432576 | tf_op jit(solution)/shard_map/yk,sxkc->sxyc/dot_general | solution.py:124
  225.9 11.7 %slice_subtract_fusion = (f32[1,8,512,256]{2,3,1,0:T(8,128)}, f32[1,8,512,256]{2,3,1,0:T(8,128)}) fusion(f32[2,8,1024,256]{2,3,1,0:T(8,128)} %convolution_bitcast_fusion), kind=kLoop, calls=%fused_computation.4 | loop fusion | flops 2097152 | bytes 25165824 | tf_op jit(solution)/shard_map/sub | solution.py:125
  237.6 5.7 %fusion = bf16[2,8,512,256]{2,3,1,0:T(8,128)(2,1)} fusion(f32[1,8,512,256]{2,3,1,0:T(8,128)} %get-tuple-element.6, f32[1,8,512,256]{2,3,1,0:T(8,128)} %get-tuple-element.5, bf16[2,8,512,256]{3,2,1,0:T(8,128)(2,1)S(1)} %copy-done.1, bf16[256,256]{1,0:T(8,128)(2,1)S(1)} %copy-done), kind=kOutput, calls=%fused_computation.1 | convolution fusion | flops 1080033280 | bytes 16908288 | tf_op jit(solution)/shard_map/dot_general | solution.py:72
  243.3 6.2 %copy.54 = bf16[2,8,512,256]{3,2,1,0:T(8,128)(2,1)} copy(bf16[2,8,512,256]{2,3,1,0:T(8,128)(2,1)} %fusion) | data formatting | bytes 8388608 | tf_op jit(solution)/shard_map/convert_element_type | solution.py:127
  (18 shorter events, 0.2 us)
Async XLA Ops:
  6.5 231.1 %copy-start = (bf16[256,256]{1,0:T(8,128)(2,1)S(1)}, bf16[256,256]{1,0:T(8,128)(2,1)}, u32[]{:S(2)}) copy-start(bf16[256,256]{1,0:T(8,128)(2,1)} %param.5) | copy-start | bytes 393220
  6.6 201.1 %all-gather.3.cloned.1.call-start = ((), (), s32[]{:S(2)}) async-start(), calls=%async_computation.3 | async-start | bytes 1572864 | tf_op jit(solution)/shard_map/all_gather | solution.py:45
  225.9 11.7 %copy-start.1 = (bf16[2,8,512,256]{3,2,1,0:T(8,128)(2,1)S(1)}, bf16[2,8,512,256]{3,2,1,0:T(8,128)(2,1)}, u32[]{:S(2)}) copy-start(bf16[2,8,512,256]{3,2,1,0:T(8,128)(2,1)} %param.3) | copy-start | bytes 12582916
Sparse Core Ops, SparseCore 0:
  180.7 26.8 all-gather.2
where the time goes:
time: 257 us; the launch traced here: 256 us
  blocking collectives  152 us (59%)
  matrix products  32.7 us (13%)
  waiting for transfers between devices  26.5 us (10%)
  local copies, waits for them, and re-layouts  18.8 us (7%)
  between operations  13.6 us (5%)
  other arithmetic  13.2 us (5%)
    all_to_all x1, blocking collectives, shards(): lax.all_to_all(outgoing.astype(jnp.bfloat16), SPACE, split_axis=2, concat...  75.3 us
    all_gather x1, blocking collectives, stacked_from(): blocks = lax.all_gather(blocks, axes[k])  45.7 us
    all_to_all x2, blocking collectives, moved_by_axis(): filled = lax.all_to_all(filled, axes[k], k, k, tiled=True)  30.6 us
    all_gather x1, waiting for transfers between devices, stacked_from(): blocks = lax.all_gather(blocks, axes[k])  26.4 us
    dot_general x1, matrix products, shards(): yback = jnp.einsum('yk,sxkc->sxyc', gy_table, slab, precision=highest)  16 us
    sub x1, other arithmetic, shards(): out_re = yback[0, :, :NY] - yback[1, :, NY:]  11.7 us
    unnamed x6, local copies, waits for them, and re-layouts  7.86 us
    dot_general x1, matrix products, shards(): jnp.einsum('ky,sxync->sxnkc', fy_table, split_field, preferred_element_ty...  7.07 us
  transfers between devices with their start and end apart: 1, of which 1 were waited for; matrix products, arithmetic and copies ran while one was open for 0% of the time, Pallas kernels for 0%

commit v1 on v0

v1 whole, which is shorter than its diff:
```python
import functools
import math

import jax
import jax.numpy as jnp
import numpy as np
from jax import lax
from jax.experimental import pallas as pl
from jax.experimental.pallas import tpu as pltpu
from jax.sharding import PartitionSpec as P

KX = 32
KY = 32
HALF = KY // 2
CHUNK = 2 * HALF
MESH = pl.DeviceIdType.MESH
F32 = jnp.float32
BF16 = jnp.bfloat16
NEAR = (2, 1, -1)
FAR = (4, 3, -3, 2, -2, 1, -1, 0)


def frequency_of(index, length, kept):
    return np.where(index < kept // 2, index, length - kept + index)


def np_table(kept, length):
    frequency = frequency_of(np.arange(kept), length, kept)
    phase = (frequency[:, None] * np.arange(length)[None, :]) % length
    angle = 2.0 * np.pi / length * phase
    return np.cos(angle) * length**-0.5, np.sin(angle) * length**-0.5


def by_half(table):
    re, im = table
    rows = [part[h * HALF : (h + 1) * HALF] for h in (0, 1) for part in (re, im)]
    return np.concatenate(rows, axis=0)


def forward_y_table(ny):
    cos, sin = np_table(KY, ny)
    from_re = by_half((cos, -sin))
    from_im = by_half((sin, cos))
    return np.stack([from_re, from_im])


def inverse_y_table(ny):
    cos, sin = np_table(KY, ny)
    to_re = by_half((cos, -sin)).T
    to_im = by_half((sin, cos)).T
    return np.stack([to_re, to_im])


def x_waves(kx, position, nx):
    frequency = jnp.where(kx < KX // 2, kx, nx - KX + kx)
    phase = frequency * position % nx
    angle = 2.0 * math.pi / nx * phase.astype(F32)
    return jnp.cos(angle) * nx**-0.5, jnp.sin(angle) * nx**-0.5


def x_position(row, local, chip, core):
    own = row < local
    place = jnp.where(own, core * local + row, (1 - core) * local + row - local)
    return chip * 2 * local + place


def forward_x_rows(local, nx, chip, core):
    shape = (2 * KX, 2 * local * CHUNK)
    b = lax.broadcasted_iota(jnp.int32, shape, 0)
    q = lax.broadcasted_iota(jnp.int32, shape, 1)
    cos, sin = x_waves(b // 2, x_position(q // CHUNK, local, chip, core), nx)
    to, of = b % 2, q // HALF % 2
    return jnp.where(to == of, cos, jnp.where(to == 0, sin, -sin))


def inverse_x_rows(local, nx, chip, core):
    shape = (4 * local, KX * CHUNK)
    b = lax.broadcasted_iota(jnp.int32, shape, 0)
    q = lax.broadcasted_iota(jnp.int32, shape, 1)
    cos, sin = x_waves(q // CHUNK, x_position(b // 2, local, chip, core), nx)
    to, of = b % 2, q // HALF % 2
    return jnp.where(to == of, cos, jnp.where(to == 0, -sin, sin))


def spread(rows_ref, full_ref):
    count, width = rows_ref.shape
    ky = lax.broadcasted_iota(jnp.int32, (HALF, width), 0)
    column = jnp.bitwise_and(lax.broadcasted_iota(jnp.int32, (HALF, width), 1), HALF - 1)
    keep = ky == column

    def one(b, carry):
        row = jnp.broadcast_to(rows_ref[pl.ds(b, 1), :], (HALF, width))
        at = pl.multiple_of(b * HALF, HALF)
        full_ref[pl.ds(at, HALF), :] = jnp.where(keep, row, 0.0).astype(BF16)
        return carry

    lax.fori_loop(0, count, one, 0)


def spectral_kernel(
    chips,
    field_ref,
    weight_ref,
    fy_ref,
    fx_ref,
    gx_ref,
    out_ref,
    fbuf,
    wbuf,
    fbig,
    gbig,
    ybuf,
    yfrom,
    parts,
    near,
    relay,
    final,
    sums,
    modes,
    zsend,
    zfrom,
    field_sem,
    weight_sem,
    ssem,
    rsem,
):
    local = fbuf.shape[0]
    me = lax.axis_index("space")
    chip, core = me // 2, lax.rem(me, 2)
    sigma = 1 - 2 * core
    used = [0]
    started = []

    def at(step):
        return lax.rem(chip + sigma * step + 2 * chips, chips)

    def copy(src, dst, device):
        k = used[0]
        used[0] += 1
        made = pltpu.make_async_remote_copy(
            src_ref=src,
            dst_ref=dst,
            send_sem=ssem.at[k],
            recv_sem=rsem.at[k],
            device_id={"space": device},
            device_id_type=MESH,
        )
        started.append(made)
        return made

    def to_chip(src, dst, step):
        return copy(src, dst, 2 * at(step) + core)

    loads = []
    for x in range(local):
        load = pltpu.make_async_copy(field_ref.at[:, x], fbuf.at[x], field_sem.at[x])
        load.start()
        loads.append(load)
    weights = pltpu.make_async_copy(weight_ref, wbuf, weight_sem)
    weights.start()

    barrier = pltpu.get_barrier_semaphore()
    for step in (1, -1, 2, -2, 4, -4, 8, -8):
        pl.semaphore_signal(
            barrier, 1, device_id={"space": 2 * at(step) + core}, device_id_type=MESH
        )
    partner = 2 * chip + 1 - core
    pl.semaphore_signal(barrier, 1, device_id={"space": partner}, device_id_type=MESH)

    spread(fx_ref, fbig)

    for x in range(local):
        loads[x].wait()
        rows = jnp.dot(fy_ref[0], fbuf[x, 0], preferred_element_type=F32)
        rows += jnp.dot(fy_ref[1], fbuf[x, 1], preferred_element_type=F32)
        rows = rows.astype(BF16)
        ybuf[0, x] = rows[:CHUNK]
        ybuf[1, x] = rows[CHUNK:]

    pl.semaphore_wait(barrier, 9)
    swap = copy(ybuf.at[1 - core], yfrom, partner)
    swap.start()
    width = ybuf.shape[-1]
    half = local * CHUNK
    own_rows = ybuf[core].reshape(half, width)
    swap.wait_recv()
    other_rows = yfrom[...].reshape(half, width)
    block = 8 * CHUNK
    for b in range(KX * CHUNK // block):
        here = pl.ds(b * block, block)
        part = jnp.dot(fbig[here, :half], own_rows, preferred_element_type=F32)
        part += jnp.dot(fbig[here, half:], other_rows, preferred_element_type=F32)
        parts[b * 8 : (b + 1) * 8] = part.astype(BF16).reshape(8, CHUNK, width)

    arrivals = {}
    for t, step in enumerate(FAR):
        for o, off in enumerate(NEAR):
            sent = to_chip(parts.at[at(4 * step - off)], near.at[o, t], -off)
            sent.start()
            arrivals[o, t] = sent

    spread(gx_ref, gbig)

    def near_sum(t):
        total = parts[at(4 * FAR[t])].astype(F32)
        for o in range(len(NEAR)):
            arrivals[o, t].wait_recv()
            total += near[o, t].astype(F32)
        return total

    def pass_on(t, total, dst, step):
        sums[t] = total.astype(BF16)
        sent = to_chip(sums.at[t], dst, step)
        sent.start()
        return sent

    relay_4 = pass_on(0, near_sum(0), relay.at[0], -8)
    relay_3 = pass_on(1, near_sum(1), relay.at[1], 4)
    relay_m3 = pass_on(2, near_sum(2), relay.at[2], -4)
    total_2, total_m2 = near_sum(3), near_sum(4)
    final_1 = pass_on(5, near_sum(5), final.at[2], 4)
    final_m1 = pass_on(6, near_sum(6), final.at[3], -4)
    mine = near_sum(7)
    relay_3.wait_recv()
    final_2 = pass_on(3, total_2 + relay[1].astype(F32), final.at[0], 8)
    relay_m3.wait_recv()
    total_m2 += relay[2].astype(F32)
    relay_4.wait_recv()
    final_m2 = pass_on(4, total_m2 + relay[0].astype(F32), final.at[1], -8)
    final_1.wait_recv()
    mine += final[2].astype(F32)
    final_m1.wait_recv()
    mine += final[3].astype(F32)
    weights.wait()
    final_2.wait_recv()
    mine += final[0].astype(F32)
    final_m2.wait_recv()
    mine += final[1].astype(F32)

    ky = jnp.bitwise_and(lax.broadcasted_iota(jnp.int32, mine.shape, 0), HALF - 1)
    by_re = jnp.zeros(mine.shape, F32)
    by_im = jnp.zeros(mine.shape, F32)
    for m in range(HALF):
        row = jnp.where(ky == m, mine, 0.0).astype(BF16)
        by_re += jnp.dot(row, wbuf[m, 0], preferred_element_type=F32)
        by_im += jnp.dot(row, wbuf[m, 1], preferred_element_type=F32)
    mixed_re = by_re[:HALF] - by_im[HALF:]
    mixed_im = by_im[:HALF] + by_re[HALF:]
    modes[chip] = jnp.concatenate([mixed_re, mixed_im], axis=0).astype(BF16)

    gathered = []

    def share(slot, step):
        sent = to_chip(modes.at[slot], modes.at[slot], step)
        sent.start()
        return sent

    def serve(slot):
        for off in NEAR:
            gathered.append(share(slot, off))

    go_2 = share(chip, 8)
    go_m2 = share(chip, -8)
    go_1 = share(chip, 4)
    go_m1 = share(chip, -4)
    serve(chip)

    go_1.wait_recv()
    serve(at(-4))
    go_m1.wait_recv()
    serve(at(4))
    go_2.wait_recv()
    go_4 = share(at(-8), 8)
    go_3 = share(at(-8), 4)
    serve(at(-8))
    go_m2.wait_recv()
    go_m3 = share(at(8), -4)
    serve(at(8))
    go_3.wait_recv()
    serve(at(-12))
    go_m3.wait_recv()
    serve(at(12))
    go_4.wait_recv()
    serve(at(-16))
    for sent in gathered:
        sent.wait_recv()

    all_modes = modes[...].reshape(KX * CHUNK, width)
    other = jnp.dot(gbig[half:, :], all_modes, preferred_element_type=F32)
    zsend[...] = other.astype(BF16).reshape(local, CHUNK, width)
    back = copy(zsend, zfrom, partner)
    back.start()
    own = jnp.dot(gbig[:half, :], all_modes, preferred_element_type=F32)
    out_ref[:, core] = own.astype(BF16).reshape(local, CHUNK, width)
    back.wait_recv()
    out_ref[:, 1 - core] = zfrom[...]
    for sent in started:
        sent.wait_send()


def finish_kernel(field_ref, z_ref, skip_ref, gy_ref, out_ref):
    z = z_ref[0].reshape(2 * CHUNK, z_ref.shape[-1])
    z = jnp.concatenate([z, z], axis=0)
    skip = skip_ref[...]
    for part in (0, 1):
        spectral = jnp.dot(gy_ref[part], z, preferred_element_type=F32)
        total = spectral + jnp.dot(field_ref[part, 0], skip, preferred_element_type=F32)
        out_ref[part, 0] = total.astype(BF16)


def shards(field, spectral_weight, skip_weight):
    devices = lax.axis_size("space")
    chips = devices // 2
    _, local, ny, width = field.shape
    nx = local * devices
    assert spectral_weight.shape[0] == HALF and chips == KX
    me = lax.axis_index("space")
    chip, core = me // 2, lax.rem(me, 2)
    fy = jnp.asarray(forward_y_table(ny), BF16)
    gy = inverse_y_table(ny).astype(np.float32)
    gy_high = np.asarray(gy.astype(jnp.bfloat16), np.float32)
    gy = jnp.asarray(np.concatenate([gy_high, gy - gy_high], axis=2), BF16)
    fx = forward_x_rows(local, nx, chip, core)
    gx = inverse_x_rows(local, nx, chip, core)
    vmem = pl.BlockSpec(memory_space=pltpu.VMEM)
    hbm = pl.BlockSpec(memory_space=pl.ANY)
    copies = 2 + 2 * (len(NEAR) * len(FAR) + len(FAR) - 1)
    z = pl.pallas_call(
        functools.partial(spectral_kernel, chips),
        out_shape=jax.ShapeDtypeStruct((local, 2, CHUNK, width), BF16),
        in_specs=[hbm, hbm, vmem, vmem, vmem],
        out_specs=vmem,
        scratch_shapes=[
            pltpu.VMEM((local, 2, ny, width), BF16),
            pltpu.VMEM(spectral_weight.shape, BF16),
            pltpu.VMEM((KX * CHUNK, 2 * local * CHUNK), BF16),
            pltpu.VMEM((2 * local * CHUNK, KX * CHUNK), BF16),
            pltpu.VMEM((2, local, CHUNK, width), BF16),
            pltpu.VMEM((local, CHUNK, width), BF16),
            pltpu.VMEM((KX, CHUNK, width), BF16),
            pltpu.VMEM((len(NEAR), len(FAR), CHUNK, width), BF16),
            pltpu.VMEM((3, CHUNK, width), BF16),
            pltpu.VMEM((4, CHUNK, width), BF16),
            pltpu.VMEM((len(FAR), CHUNK, width), BF16),
            pltpu.VMEM((KX, CHUNK, width), BF16),
            pltpu.VMEM((local, CHUNK, width), BF16),
            pltpu.VMEM((local, CHUNK, width), BF16),
            pltpu.SemaphoreType.DMA((local,)),
            pltpu.SemaphoreType.DMA,
            pltpu.SemaphoreType.DMA((copies,)),
            pltpu.SemaphoreType.DMA((copies,)),
        ],
        name="spectral",
        compiler_params=pltpu.CompilerParams(collective_id=1, has_side_effects=True),
    )(field, spectral_weight, fy, fx, gx)
    rows = pl.BlockSpec((2, 1, ny, width), lambda x: (0, x, 0, 0))
    return pl.pallas_call(
        finish_kernel,
        grid=(local,),
        out_shape=jax.ShapeDtypeStruct(field.shape, BF16),
        in_specs=[
            rows,
            pl.BlockSpec((1, 2, CHUNK, width), lambda x: (x, 0, 0, 0)),
            pl.BlockSpec((width, width), lambda x: (0, 0)),
            pl.BlockSpec(gy.shape, lambda x: (0, 0, 0)),
        ],
        out_specs=rows,
        name="finish",
    )(field, z, skip_weight, gy)


def solution(mesh):
    return jax.shard_map(
        shards,
        mesh=mesh,
        in_specs=(P("group", "space", None, None), P("space", None, None, None), P()),
        out_specs=P("group", "space", None, None),
        check_vma=False,
    )
```

time: 257 us -> 86.5 us (0.34)
  blocking collectives: 152 us -> 0 us
  Pallas kernels: 0 us -> 83.5 us
  matrix products: 32.7 us -> 0 us
  waiting for transfers between devices: 26.5 us -> 0 us
  local copies, waits for them, and re-layouts: 18.8 us -> 0 us
  between operations: 13.6 us -> 0.08 us
  other arithmetic: 13.2 us -> 2.69 us
    all_to_all x3 -> x0, blocking collectives: 106 us -> none  [the longest x1 75.3 us: shards(): lax.all_to_all(outgoing.astype(jnp.bfloat16), SPACE, split_axis=2, concat...]
    pallas_call x0 -> x2, Pallas kernels: none -> 83.5 us  [the longest x1 75.3 us: shards(): pl.pallas_call(functools.partial(spectral_kernel, chips), out_shape=jax.S...]
    all_gather x1 -> x0, blocking collectives: 45.7 us -> none  [stacked_from(): blocks = lax.all_gather(blocks, axes[k])]
    dot_general x7 -> x0, matrix products: 32.7 us -> none  [the longest x1 16 us: shards(): yback = jnp.einsum('yk,sxkc->sxyc', gy_table, slab, precision=highest)]
    all_gather x1 -> x0, waiting for transfers between devices: 26.4 us -> none  [stacked_from(): blocks = lax.all_gather(blocks, axes[k])]
    sub x2 -> x4, other arithmetic: 11.8 us -> 0.02 us  [the longest x2 0.01 us: forward_x_rows(): cos, sin = x_waves(b // 2, x_position(q // CHUNK, local, chip, core), nx)]
    unnamed x6 -> x0, local copies, waits for them, and re-layouts: 7.86 us -> none
    convert_element_type x2 -> x0, local copies, waits for them, and re-layouts: 6.27 us -> none  [the longest x1 6.19 us: shards(): return (jnp.stack([out_re, out_im]) + skip_part).astype(jnp.bfloat16)]
  transfers between devices with their start and end apart: 1 -> 0, of which waited for: 1 -> 0; matrix products, arithmetic and copies ran while one was open for 0% -> 0% of each run, Pallas kernels for 0% -> 0%
where the time goes in v1:
time: 86.5 us; the launch traced here: 86.3 us
  Pallas kernels  83.5 us (97%)
  other arithmetic  2.69 us (3%)
    pallas_call x1, Pallas kernels, shards(): pl.pallas_call(functools.partial(spectral_kernel, chips), out_shape=jax.S...  75.3 us
    pallas_call x1, Pallas kernels, shards(): pl.pallas_call(finish_kernel, grid=(local,), out_shape=jax.ShapeDtypeStru...  8.15 us

profile of v1, /device:TPU:37, one launch (start us, length us, event | category | flops | bytes accessed | tf_op | source)
XLA Modules:
  0.0 86.3 jit_solution(7900165202442617455)
XLA Ops:
  0.1 1.3 %fusion.7.gx_ref = f32[32,1024]{1,0:T(8,128)} fusion(s32[]{:T(128)S(6)} %mul.46, s32[]{:T(128)S(6)} %mul.45, s32[32]{0:T(128)S(1)} %get-tuple-element.25, s32[32]{0:T(128)S(1)} %get-tuple-element.27, s32[]{:T(128)S(6)} %mul.44, s32[1024]{0:T(1024)S(1)} %get-tuple-element.18, s32[1024]{0:T(1024)S(1)} %get-tuple-element.21, s32[1024]{0:T(1024)S(1)} %get-tuple-element.17, ...), kind=kLoop, calls=%fused_computation.37 | loop fusion | flops 1474560 | bytes 150092 | tf_op jit(solution)/shard_map/jit(_where)/select_n | solution.py:82
  1.4 1.3 %fusion.3.fx_ref = f32[64,512]{1,0:T(8,128)} fusion(s32[]{:T(128)S(6)} %mul.46, s32[]{:T(128)S(6)} %mul.45, s32[512]{0:T(512)S(1)} %get-tuple-element.6, s32[512]{0:T(512)S(1)} %get-tuple-element.11, s32[]{:T(128)S(6)} %mul.44, s32[64]{0:T(128)S(1)} %get-tuple-element.13, s32[64]{0:T(128)S(1)} %get-tuple-element.15, s32[512]{0:T(512)S(1)} %get-tuple-element.5, ...), kind=kLoop, calls=%fused_computation.33 | loop fusion | flops 1474560 | bytes 141452 | tf_op jit(solution)/shard_map/jit(_where)/select_n | solution.py:73
  2.8 75.3 %spectral.1.z_ref = bf16[8,2,32,256]{3,2,1,0:T(8,128)(2,1)} custom-call(bf16[2,8,512,256]{3,2,1,0:T(8,128)(2,1)} %field_ref.3, bf16[16,2,256,256]{3,2,1,0:T(8,128)(2,1)} %weight_ref.1, bf16[2,64,512]{2,1,0:T(8,128)(2,1)} %constant.163.clone.fy_ref, f32[64,512]{1,0:T(8,128)} %fusion.3.fx_ref, f32[32,1024]{1,0:T(8,128)} %fusion.7.gx_ref), custom_call_target="tpu_custom_call" | custom-call | tf_op jit(solution)/shard_map/spectral/pallas_call | solution.py:328
  78.1 8.2 %finish.1 = bf16[2,8,512,256]{3,2,1,0:T(8,128)(2,1)} custom-call(bf16[2,8,512,256]{3,2,1,0:T(8,128)(2,1)} %field_ref.3, bf16[8,2,32,256]{3,2,1,0:T(8,128)(2,1)} %spectral.1.z_ref, bf16[256,256]{1,0:T(8,128)(2,1)} %skip_ref.1, bf16[2,512,128]{2,1,0:T(8,128)(2,1)} %constant.164.clone.gy_ref), custom_call_target="tpu_custom_call" | custom-call | tf_op jit(solution)/shard_map/finish/pallas_call | solution.py:357
  (12 shorter events, 0.1 us)

commit v2 on v1

--- a/solution.py
+++ b/solution.py
@@ -1,5 +1,4 @@
 import functools
-import math
 
 import jax
 import jax.numpy as jnp
@@ -13,10 +12,13 @@
 KY = 32
 HALF = KY // 2
 CHUNK = 2 * HALF
+ROWS = 2
+FIRST_VMEM = 26 << 20
+LAST_VMEM = 14 << 20
 MESH = pl.DeviceIdType.MESH
 F32 = jnp.float32
 BF16 = jnp.bfloat16
-NEAR = (2, 1, -1)
+NEAR = (-2, -1, 1)
 FAR = (4, 3, -3, 2, -2, 1, -1, 0)
 
 
@@ -51,39 +53,30 @@
     return np.stack([to_re, to_im])
 
 
-def x_waves(kx, position, nx):
-    frequency = jnp.where(kx < KX // 2, kx, nx - KX + kx)
-    phase = frequency * position % nx
-    angle = 2.0 * math.pi / nx * phase.astype(F32)
-    return jnp.cos(angle) * nx**-0.5, jnp.sin(angle) * nx**-0.5
-
-
-def x_position(row, local, chip, core):
-    own = row < local
-    place = jnp.where(own, core * local + row, (1 - core) * local + row - local)
-    return chip * 2 * local + place
-
-
-def forward_x_rows(local, nx, chip, core):
-    shape = (2 * KX, 2 * local * CHUNK)
-    b = lax.broadcasted_iota(jnp.int32, shape, 0)
-    q = lax.broadcasted_iota(jnp.int32, shape, 1)
-    cos, sin = x_waves(b // 2, x_position(q // CHUNK, local, chip, core), nx)
-    to, of = b % 2, q // HALF % 2
-    return jnp.where(to == of, cos, jnp.where(to == 0, sin, -sin))
-
-
-def inverse_x_rows(local, nx, chip, core):
-    shape = (4 * local, KX * CHUNK)
-    b = lax.broadcasted_iota(jnp.int32, shape, 0)
-    q = lax.broadcasted_iota(jnp.int32, shape, 1)
-    cos, sin = x_waves(q // CHUNK, x_position(b // 2, local, chip, core), nx)
-    to, of = b % 2, q // HALF % 2
-    return jnp.where(to == of, cos, jnp.where(to == 0, -sin, sin))
-
-
-def spread(rows_ref, full_ref):
+def x_tables(local, devices):
+    nx = local * devices
+    cos, sin = np_table(KX, nx)
+    tables = np.zeros((devices, 2 * KX + 4 * local, 2 * KX))
+    for device in range(devices):
+        chip, core = divmod(device, 2)
+        rows = [np.arange(local) + (2 * chip + side) * local for side in (core, 1 - core)]
+        rows = np.concatenate(rows)
+        c, s = cos[:, rows], sin[:, rows]
+        forward = np.stack([np.stack([c, s], -1), np.stack([-s, c], -1)], 1)
+        forward = forward.reshape(2 * KX, 4 * local)
+        tables[device, : 2 * KX, : 4 * local] = forward
+        tables[device, 2 * KX :] = forward.T
+    return tables
+
+
+def spread(table, rows_ref, full_ref):
     count, width = rows_ref.shape
+    shape = (table.shape[1], width)
+    one_hot = lax.broadcasted_iota(jnp.int32, shape, 0) == lax.shift_right_logical(
+        lax.broadcasted_iota(jnp.int32, shape, 1), HALF.bit_length() - 1
+    )
+    one_hot = jnp.where(one_hot, 1.0, 0.0).astype(BF16)
+    rows_ref[...] = jnp.dot(table, one_hot, preferred_element_type=F32)
     ky = lax.broadcasted_iota(jnp.int32, (HALF, width), 0)
     column = jnp.bitwise_and(lax.broadcasted_iota(jnp.int32, (HALF, width), 1), HALF - 1)
     keep = ky == column
@@ -94,19 +87,25 @@
         full_ref[pl.ds(at, HALF), :] = jnp.where(keep, row, 0.0).astype(BF16)
         return carry
 
-    lax.fori_loop(0, count, one, 0)
+    lax.fori_loop(0, count, one, 0, unroll=4)
 
 
 def spectral_kernel(
     chips,
     field_ref,
     weight_ref,
-    fy_ref,
-    fx_ref,
-    gx_ref,
+    skip_hbm,
+    fy_hbm,
+    table_ref,
     out_ref,
+    skipped_ref,
     fbuf,
     wbuf,
+    skip_ref,
+    fy_ref,
+    tbuf,
+    frows,
+    grows,
     fbig,
     gbig,
     ybuf,
@@ -121,8 +120,12 @@
     zfrom,
     field_sem,
     weight_sem,
+    table_sem,
+    fy_sem,
+    skip_sem,
     ssem,
     rsem,
+    far_sem,
 ):
     local = fbuf.shape[0]
     me = lax.axis_index("space")
@@ -151,6 +154,10 @@
     def to_chip(src, dst, step):
         return copy(src, dst, 2 * at(step) + core)
 
+    table = pltpu.make_async_copy(table_ref.at[me], tbuf, table_sem)
+    table.start()
+    waves = pltpu.make_async_copy(fy_hbm, fy_ref, fy_sem)
+    waves.start()
     loads = []
     for x in range(local):
         load = pltpu.make_async_copy(field_ref.at[:, x], fbuf.at[x], field_sem.at[x])
@@ -158,17 +165,21 @@
         loads.append(load)
     weights = pltpu.make_async_copy(weight_ref, wbuf, weight_sem)
     weights.start()
+    skip = pltpu.make_async_copy(skip_hbm, skip_ref, skip_sem)
+    skip.start()
 
     barrier = pltpu.get_barrier_semaphore()
-    for step in (1, -1, 2, -2, 4, -4, 8, -8):
+    for step in (4, -4, 2, -2, 1, -1):
         pl.semaphore_signal(
             barrier, 1, device_id={"space": 2 * at(step) + core}, device_id_type=MESH
         )
     partner = 2 * chip + 1 - core
     pl.semaphore_signal(barrier, 1, device_id={"space": partner}, device_id_type=MESH)
 
-    spread(fx_ref, fbig)
-
+    table.wait()
+    spread(tbuf[: 2 * KX], frows, fbig)
+
+    waves.wait()
     for x in range(local):
         loads[x].wait()
         rows = jnp.dot(fy_ref[0], fbuf[x, 0], preferred_element_type=F32)
@@ -177,7 +188,11 @@
         ybuf[0, x] = rows[:CHUNK]
         ybuf[1, x] = rows[CHUNK:]
 
-    pl.semaphore_wait(barrier, 9)
+    pl.semaphore_wait(barrier, 7)
+    for step in (4, -4):
+        pl.semaphore_signal(
+            far_sem, 1, device_id={"space": 2 * at(step) + core}, device_id_type=MESH
+        )
     swap = copy(ybuf.at[1 - core], yfrom, partner)
     swap.start()
     width = ybuf.shape[-1]
@@ -199,7 +214,7 @@
             sent.start()
             arrivals[o, t] = sent
 
-    spread(gx_ref, gbig)
+    spread(tbuf[2 * KX :], grows, gbig)
 
     def near_sum(t):
         total = parts[at(4 * FAR[t])].astype(F32)
@@ -214,6 +229,7 @@
         sent.start()
         return sent
 
+    pl.semaphore_wait(far_sem, 2)
     relay_4 = pass_on(0, near_sum(0), relay.at[0], -8)
     relay_3 = pass_on(1, near_sum(1), relay.at[1], 4)
     relay_m3 = pass_on(2, near_sum(2), relay.at[2], -4)
@@ -221,6 +237,17 @@
     final_1 = pass_on(5, near_sum(5), final.at[2], 4)
     final_m1 = pass_on(6, near_sum(6), final.at[3], -4)
     mine = near_sum(7)
+
+    skip.wait()
+
+    def skip_rows(n, carry):
+        x, part = n // 2, lax.rem(n, 2)
+        skipped_ref[x, part] = jnp.dot(
+            fbuf[x, part], skip_ref[...], preferred_element_type=F32
+        )
+        return carry
+
+    lax.fori_loop(0, 2 * local, skip_rows, 0)
     relay_3.wait_recv()
     final_2 = pass_on(3, total_2 + relay[1].astype(F32), final.at[0], 8)
     relay_m3.wait_recv()
@@ -298,41 +325,47 @@
         sent.wait_send()
 
 
-def finish_kernel(field_ref, z_ref, skip_ref, gy_ref, out_ref):
-    z = z_ref[0].reshape(2 * CHUNK, z_ref.shape[-1])
-    z = jnp.concatenate([z, z], axis=0)
-    skip = skip_ref[...]
-    for part in (0, 1):
-        spectral = jnp.dot(gy_ref[part], z, preferred_element_type=F32)
-        total = spectral + jnp.dot(field_ref[part, 0], skip, preferred_element_type=F32)
-        out_ref[part, 0] = total.astype(BF16)
+def finish_kernel(skipped_ref, z_ref, gy_ref, out_ref):
+    block = out_ref.shape[1]
+    for x in range(block):
+        row = pl.program_id(0) * block + x
+        z = z_ref[row].reshape(2 * CHUNK, z_ref.shape[-1])
+        z = jnp.concatenate([z, z], axis=0)
+        for part in (0, 1):
+            spectral = jnp.dot(gy_ref[part], z, preferred_element_type=F32)
+            out_ref[part, x] = (spectral + skipped_ref[row, part]).astype(BF16)
 
 
 def shards(field, spectral_weight, skip_weight):
     devices = lax.axis_size("space")
     chips = devices // 2
     _, local, ny, width = field.shape
-    nx = local * devices
     assert spectral_weight.shape[0] == HALF and chips == KX
-    me = lax.axis_index("space")
-    chip, core = me // 2, lax.rem(me, 2)
     fy = jnp.asarray(forward_y_table(ny), BF16)
     gy = inverse_y_table(ny).astype(np.float32)
     gy_high = np.asarray(gy.astype(jnp.bfloat16), np.float32)
     gy = jnp.asarray(np.concatenate([gy_high, gy - gy_high], axis=2), BF16)
-    fx = forward_x_rows(local, nx, chip, core)
-    gx = inverse_x_rows(local, nx, chip, core)
+    tables = jnp.asarray(x_tables(local, devices), BF16)
     vmem = pl.BlockSpec(memory_space=pltpu.VMEM)
-    hbm = pl.BlockSpec(memory_space=pl.ANY)
+    hbm = pl.BlockSpec(memory_space=pltpu.HBM)
     copies = 2 + 2 * (len(NEAR) * len(FAR) + len(FAR) - 1)
-    z = pl.pallas_call(
+    arrays = (field, spectral_weight, skip_weight, fy, tables)
+    z, skipped = pl.pallas_call(
         functools.partial(spectral_kernel, chips),
-        out_shape=jax.ShapeDtypeStruct((local, 2, CHUNK, width), BF16),
-        in_specs=[hbm, hbm, vmem, vmem, vmem],
-        out_specs=vmem,
+        out_shape=(
+            jax.ShapeDtypeStruct((local, 2, CHUNK, width), BF16),
+            jax.ShapeDtypeStruct((local, 2, ny, width), F32),
+        ),
+        in_specs=[hbm] * 5,
+        out_specs=(vmem, vmem),
         scratch_shapes=[
             pltpu.VMEM((local, 2, ny, width), BF16),
             pltpu.VMEM(spectral_weight.shape, BF16),
+            pltpu.VMEM(skip_weight.shape, BF16),
+            pltpu.VMEM(fy.shape, BF16),
+            pltpu.VMEM(tables.shape[1:], BF16),
+            pltpu.VMEM((2 * KX, 2 * local * CHUNK), F32),
+            pltpu.VMEM((4 * local, KX * CHUNK), F32),
             pltpu.VMEM((KX * CHUNK, 2 * local * CHUNK), BF16),
             pltpu.VMEM((2 * local * CHUNK, KX * CHUNK), BF16),
             pltpu.VMEM((2, local, CHUNK, width), BF16),
@@ -347,26 +380,27 @@
             pltpu.VMEM((local, CHUNK, width), BF16),
             pltpu.SemaphoreType.DMA((local,)),
             pltpu.SemaphoreType.DMA,
+            pltpu.SemaphoreType.DMA,
+            pltpu.SemaphoreType.DMA,
+            pltpu.SemaphoreType.DMA,
             pltpu.SemaphoreType.DMA((copies,)),
             pltpu.SemaphoreType.DMA((copies,)),
+            pltpu.SemaphoreType.REGULAR,
         ],
         name="spectral",
-        compiler_params=pltpu.CompilerParams(collective_id=1, has_side_effects=True),
-    )(field, spectral_weight, fy, fx, gx)
-    rows = pl.BlockSpec((2, 1, ny, width), lambda x: (0, x, 0, 0))
+        compiler_params=pltpu.CompilerParams(
+            collective_id=1, has_side_effects=True, vmem_limit_bytes=FIRST_VMEM
+        ),
+    )(*(pltpu.with_memory_space_constraint(array, pltpu.HBM) for array in arrays))
     return pl.pallas_call(
         finish_kernel,
-        grid=(local,),
+        grid=(local // ROWS,),
         out_shape=jax.ShapeDtypeStruct(field.shape, BF16),
-        in_specs=[
-            rows,
-            pl.BlockSpec((1, 2, CHUNK, width), lambda x: (x, 0, 0, 0)),
-            pl.BlockSpec((width, width), lambda x: (0, 0)),
-            pl.BlockSpec(gy.shape, lambda x: (0, 0, 0)),
-        ],
-        out_specs=rows,
+        in_specs=[vmem, vmem, vmem],
+        out_specs=pl.BlockSpec((2, ROWS, ny, width), lambda x: (0, x, 0, 0)),
         name="finish",
-    )(field, z, skip_weight, gy)
+        compiler_params=pltpu.CompilerParams(vmem_limit_bytes=LAST_VMEM),
+    )(skipped, z, gy)
 
 
 def solution(mesh):

time: 86.5 us -> 75.9 us (0.88)
  Pallas kernels: 83.5 us -> 75.8 us
  other arithmetic: 2.69 us -> 0 us
    pallas_call x2, Pallas kernels: 83.5 us -> 75.8 us  [the longest x1 72.6 us: shards(): pl.pallas_call(functools.partial(spectral_kernel, chips), out_shape=(jax....]
    select_n x2 -> x0, other arithmetic: 2.62 us -> none  [the longest x1 1.31 us: inverse_x_rows(): return jnp.where(to == of, cos, jnp.where(to == 0, -sin, sin))]
where the time goes in v2:
time: 75.9 us
  Pallas kernels  75.8 us (100%)
    pallas_call x1, Pallas kernels, shards(): pl.pallas_call(functools.partial(spectral_kernel, chips), out_shape=(jax....  72.6 us
    pallas_call x1, Pallas kernels, shards(): pl.pallas_call(finish_kernel, grid=(local // ROWS,), out_shape=jax.ShapeD...  3.24 us

profile of v2, /device:TPU:37, one launch (start us, length us, event | category | flops | bytes accessed | tf_op | source)
XLA Modules:
  0.0 75.9 jit_solution(6796383768851374301)
XLA Ops:
  0.0 0.0 copy-start
  0.0 72.6 %spectral.1 = (bf16[8,2,32,256]{3,2,1,0:T(8,128)(2,1)S(1)}, f32[8,2,512,256]{3,2,1,0:T(8,128)S(1)}) custom-call(bf16[2,8,512,256]{3,2,1,0:T(8,128)(2,1)} %field_ref.1, bf16[16,2,256,256]{3,2,1,0:T(8,128)(2,1)} %weight_ref.1, bf16[256,256]{1,0:T(8,128)(2,1)} %skip_hbm.1, bf16[2,64,512]{2,1,0:T(8,128)(2,1)} %constant.6.clone.fy_hbm, ...), custom_call_target="tpu_custom_call" | custom-call | tf_op jit(solution)/shard_map/spectral/pallas_call | solution.py:353
  72.6 0.0 copy-done
  72.6 3.2 %finish.1 = bf16[2,8,512,256]{3,2,1,0:T(8,128)(2,1)} custom-call(f32[8,2,512,256]{3,2,1,0:T(8,128)S(1)} %get-tuple-element.7.skipped_ref, bf16[8,2,32,256]{3,2,1,0:T(8,128)(2,1)S(1)} %get-tuple-element.8.z_ref, bf16[2,512,128]{2,1,0:T(8,128)(2,1)S(1)} %copy-done), custom_call_target="tpu_custom_call" | custom-call | tf_op jit(solution)/shard_map/finish/pallas_call | solution.py:395
Async XLA Ops:
  0.0 72.6 %copy-start = (bf16[2,512,128]{2,1,0:T(8,128)(2,1)S(1)}, bf16[2,512,128]{2,1,0:T(8,128)(2,1)}, u32[]{:S(2)}) copy-start(bf16[2,512,128]{2,1,0:T(8,128)(2,1)} %constant.7.clone.gy_ref) | copy-start | bytes 786436

commit v3 on v2

--- a/solution.py
+++ b/solution.py
@@ -18,8 +18,16 @@
 MESH = pl.DeviceIdType.MESH
 F32 = jnp.float32
 BF16 = jnp.bfloat16
-NEAR = (-2, -1, 1)
-FAR = (4, 3, -3, 2, -2, 1, -1, 0)
+HUBS = {
+    12: (4, 3, 2, -2, 1, -1),
+    -12: (-3, -2, 1, -1),
+    8: (-2, 1, -1),
+    -8: (-2, 1, -1),
+    4: (-2, 1, -1),
+    -4: (-2, 1, -1),
+    0: (-2, 1, -1),
+}
+NEAR_COPIES = sum(len(offsets) for offsets in HUBS.values())
 
 
 def frequency_of(index, length, kept):
@@ -112,7 +120,6 @@
     yfrom,
     parts,
     near,
-    relay,
     final,
     sums,
     modes,
@@ -126,6 +133,7 @@
     ssem,
     rsem,
     far_sem,
+    farther_sem,
 ):
     local = fbuf.shape[0]
     me = lax.axis_index("space")
@@ -158,21 +166,22 @@
     table.start()
     waves = pltpu.make_async_copy(fy_hbm, fy_ref, fy_sem)
     waves.start()
+
+    def signal_chip(semaphore, step):
+        device = {"space": 2 * at(step) + core}
+        pl.semaphore_signal(semaphore, 1, device_id=device, device_id_type=MESH)
+
     loads = []
     for x in range(local):
         load = pltpu.make_async_copy(field_ref.at[:, x], fbuf.at[x], field_sem.at[x])
         load.start()
         loads.append(load)
     weights = pltpu.make_async_copy(weight_ref, wbuf, weight_sem)
-    weights.start()
     skip = pltpu.make_async_copy(skip_hbm, skip_ref, skip_sem)
-    skip.start()
 
     barrier = pltpu.get_barrier_semaphore()
-    for step in (4, -4, 2, -2, 1, -1):
-        pl.semaphore_signal(
-            barrier, 1, device_id={"space": 2 * at(step) + core}, device_id_type=MESH
-        )
+    for step in (4, -4, 3, -3, 2, -2, 1, -1):
+        signal_chip(barrier, step)
     partner = 2 * chip + 1 - core
     pl.semaphore_signal(barrier, 1, device_id={"space": partner}, device_id_type=MESH)
 
@@ -188,11 +197,11 @@
         ybuf[0, x] = rows[:CHUNK]
         ybuf[1, x] = rows[CHUNK:]
 
-    pl.semaphore_wait(barrier, 7)
-    for step in (4, -4):
-        pl.semaphore_signal(
-            far_sem, 1, device_id={"space": 2 * at(step) + core}, device_id_type=MESH
-        )
+    weights.start()
+    skip.start()
+    pl.semaphore_wait(barrier, 9)
+    signal_chip(far_sem, 4)
+    signal_chip(far_sem, -4)
     swap = copy(ybuf.at[1 - core], yfrom, partner)
     swap.start()
     width = ybuf.shape[-1]
@@ -208,35 +217,37 @@
         parts[b * 8 : (b + 1) * 8] = part.astype(BF16).reshape(8, CHUNK, width)
 
     arrivals = {}
-    for t, step in enumerate(FAR):
-        for o, off in enumerate(NEAR):
-            sent = to_chip(parts.at[at(4 * step - off)], near.at[o, t], -off)
+    for hub, offsets in HUBS.items():
+        for offset in offsets:
+            slot = len(arrivals)
+            sent = to_chip(parts.at[at(-offset - hub)], near.at[slot], -offset)
             sent.start()
-            arrivals[o, t] = sent
+            arrivals[hub, offset] = sent, slot
+    pl.semaphore_wait(far_sem, 2)
+    signal_chip(farther_sem, 4)
+    signal_chip(farther_sem, -4)
 
     spread(tbuf[2 * KX :], grows, gbig)
 
-    def near_sum(t):
-        total = parts[at(4 * FAR[t])].astype(F32)
-        for o in range(len(NEAR)):
-            arrivals[o, t].wait_recv()
-            total += near[o, t].astype(F32)
+    def near_sum(hub):
+        total = parts[at(-hub)].astype(F32)
+        for offset in HUBS[hub]:
+            sent, slot = arrivals[hub, offset]
+            sent.wait_recv()
+            total += near[slot].astype(F32)
         return total
 
-    def pass_on(t, total, dst, step):
-        sums[t] = total.astype(BF16)
-        sent = to_chip(sums.at[t], dst, step)
+    pl.semaphore_wait(farther_sem, 2)
+    finals = []
+    for hub in HUBS:
+        if hub == 0:
+            continue
+        slot = len(finals)
+        sums[slot] = near_sum(hub).astype(BF16)
+        sent = to_chip(sums.at[slot], final.at[slot], -hub)
         sent.start()
-        return sent
-
-    pl.semaphore_wait(far_sem, 2)
-    relay_4 = pass_on(0, near_sum(0), relay.at[0], -8)
-    relay_3 = pass_on(1, near_sum(1), relay.at[1], 4)
-    relay_m3 = pass_on(2, near_sum(2), relay.at[2], -4)
-    total_2, total_m2 = near_sum(3), near_sum(4)
-    final_1 = pass_on(5, near_sum(5), final.at[2], 4)
-    final_m1 = pass_on(6, near_sum(6), final.at[3], -4)
-    mine = near_sum(7)
+        finals.append(sent)
+    mine = near_sum(0)
 
     skip.wait()
 
@@ -248,21 +259,10 @@
         return carry
 
     lax.fori_loop(0, 2 * local, skip_rows, 0)
-    relay_3.wait_recv()
-    final_2 = pass_on(3, total_2 + relay[1].astype(F32), final.at[0], 8)
-    relay_m3.wait_recv()
-    total_m2 += relay[2].astype(F32)
-    relay_4.wait_recv()
-    final_m2 = pass_on(4, total_m2 + relay[0].astype(F32), final.at[1], -8)
-    final_1.wait_recv()
-    mine += final[2].astype(F32)
-    final_m1.wait_recv()
-    mine += final[3].astype(F32)
     weights.wait()
-    final_2.wait_recv()
-    mine += final[0].astype(F32)
-    final_m2.wait_recv()
-    mine += final[1].astype(F32)
+    for slot in reversed(range(len(finals))):
+        finals[slot].wait_recv()
+        mine += final[slot].astype(F32)
 
     ky = jnp.bitwise_and(lax.broadcasted_iota(jnp.int32, mine.shape, 0), HALF - 1)
     by_re = jnp.zeros(mine.shape, F32)
@@ -282,33 +282,12 @@
         sent.start()
         return sent
 
-    def serve(slot):
-        for off in NEAR:
-            gathered.append(share(slot, off))
-
-    go_2 = share(chip, 8)
-    go_m2 = share(chip, -8)
-    go_1 = share(chip, 4)
-    go_m1 = share(chip, -4)
-    serve(chip)
-
-    go_1.wait_recv()
-    serve(at(-4))
-    go_m1.wait_recv()
-    serve(at(4))
-    go_2.wait_recv()
-    go_4 = share(at(-8), 8)
-    go_3 = share(at(-8), 4)
-    serve(at(-8))
-    go_m2.wait_recv()
-    go_m3 = share(at(8), -4)
-    serve(at(8))
-    go_3.wait_recv()
-    serve(at(-12))
-    go_m3.wait_recv()
-    serve(at(12))
-    go_4.wait_recv()
-    serve(at(-16))
+    shared = {hub: share(chip, hub) for hub in HUBS if hub != 0}
+    for hub in reversed(HUBS):
+        if hub != 0:
+            shared[hub].wait_recv()
+        for offset in HUBS[hub]:
+            gathered.append(share(at(-hub), offset))
     for sent in gathered:
         sent.wait_recv()
 
@@ -348,7 +327,7 @@
     tables = jnp.asarray(x_tables(local, devices), BF16)
     vmem = pl.BlockSpec(memory_space=pltpu.VMEM)
     hbm = pl.BlockSpec(memory_space=pltpu.HBM)
-    copies = 2 + 2 * (len(NEAR) * len(FAR) + len(FAR) - 1)
+    copies = 2 + 2 * (NEAR_COPIES + len(HUBS) - 1)
     arrays = (field, spectral_weight, skip_weight, fy, tables)
     z, skipped = pl.pallas_call(
         functools.partial(spectral_kernel, chips),
@@ -371,10 +350,9 @@
             pltpu.VMEM((2, local, CHUNK, width), BF16),
             pltpu.VMEM((local, CHUNK, width), BF16),
             pltpu.VMEM((KX, CHUNK, width), BF16),
-            pltpu.VMEM((len(NEAR), len(FAR), CHUNK, width), BF16),
-            pltpu.VMEM((3, CHUNK, width), BF16),
-            pltpu.VMEM((4, CHUNK, width), BF16),
-            pltpu.VMEM((len(FAR), CHUNK, width), BF16),
+            pltpu.VMEM((NEAR_COPIES, CHUNK, width), BF16),
+            pltpu.VMEM((len(HUBS) - 1, CHUNK, width), BF16),
+            pltpu.VMEM((len(HUBS) - 1, CHUNK, width), BF16),
             pltpu.VMEM((KX, CHUNK, width), BF16),
             pltpu.VMEM((local, CHUNK, width), BF16),
             pltpu.VMEM((local, CHUNK, width), BF16),
@@ -385,6 +363,7 @@
             pltpu.SemaphoreType.DMA,
             pltpu.SemaphoreType.DMA((copies,)),
             pltpu.SemaphoreType.DMA((copies,)),
+            pltpu.SemaphoreType.REGULAR,
             pltpu.SemaphoreType.REGULAR,
         ],
         name="spectral",

time: 75.9 us -> 74.9 us (0.987)
  Pallas kernels: 75.8 us -> 74.8 us
    pallas_call x1, Pallas kernels: 72.6 us -> 71.6 us  [shards(): pl.pallas_call(functools.partial(spectral_kernel, chips), out_shape=(jax....]
where the time goes in v3:
time: 74.9 us; the launch traced here: 74.8 us
  Pallas kernels  74.8 us (100%)
    pallas_call x1, Pallas kernels, shards(): pl.pallas_call(functools.partial(spectral_kernel, chips), out_shape=(jax....  71.6 us
    pallas_call x1, Pallas kernels, shards(): pl.pallas_call(finish_kernel, grid=(local // ROWS,), out_shape=jax.ShapeD...  3.23 us

profile of v3, /device:TPU:37, one launch (start us, length us, event | category | flops | bytes accessed | tf_op | source)
XLA Modules:
  0.0 74.8 jit_solution(5046225369875025260)
XLA Ops:
  0.0 0.0 copy-start
  0.0 71.6 %spectral.1 = (bf16[8,2,32,256]{3,2,1,0:T(8,128)(2,1)S(1)}, f32[8,2,512,256]{3,2,1,0:T(8,128)S(1)}) custom-call(bf16[2,8,512,256]{3,2,1,0:T(8,128)(2,1)} %field_ref.1, bf16[16,2,256,256]{3,2,1,0:T(8,128)(2,1)} %weight_ref.1, bf16[256,256]{1,0:T(8,128)(2,1)} %skip_hbm.1, bf16[2,64,512]{2,1,0:T(8,128)(2,1)} %constant.6.clone.fy_hbm, ...), custom_call_target="tpu_custom_call" | custom-call | tf_op jit(solution)/shard_map/spectral/pallas_call | solution.py:332
  71.6 0.0 copy-done
  71.6 3.2 %finish.1 = bf16[2,8,512,256]{3,2,1,0:T(8,128)(2,1)} custom-call(f32[8,2,512,256]{3,2,1,0:T(8,128)S(1)} %get-tuple-element.7.skipped_ref, bf16[8,2,32,256]{3,2,1,0:T(8,128)(2,1)S(1)} %get-tuple-element.8.z_ref, bf16[2,512,128]{2,1,0:T(8,128)(2,1)S(1)} %copy-done), custom_call_target="tpu_custom_call" | custom-call | tf_op jit(solution)/shard_map/finish/pallas_call | solution.py:374
Async XLA Ops:
  0.0 71.6 %copy-start = (bf16[2,512,128]{2,1,0:T(8,128)(2,1)S(1)}, bf16[2,512,128]{2,1,0:T(8,128)(2,1)}, u32[]{:S(2)}) copy-start(bf16[2,512,128]{2,1,0:T(8,128)(2,1)} %constant.7.clone.gy_ref) | copy-start | bytes 786436
